TPU v7x, 8 devices: a whole 2x2x1 slice. The times are simulated.
8 devices in a mesh: dp: 1 (over z), a: 2 (over y), b: 4 (over x, core).
Axes of the slice: x: 2, y: 2, z: 1, core: 2. Of those that a mesh axis runs over, the one named last changes fastest.
Arguments:
- x: bfloat16 [2048, 8192], P('dp', ('a', 'b'))
- w_gate: bfloat16 [8192, 22016], P('a', 'b')
- w_up: bfloat16 [8192, 22016], P('a', 'b')
- w_down: bfloat16 [22016, 8192], P('b', 'a')
Outputs:
- output: bfloat16 [2048, 8192], P('dp', ('a', 'b'))
All inputs are finite; a program needn't handle non-finite values.
Results may differ from a plain program's by a relative error of at most 0.016.
Values are sent between devices in bfloat16 or wider.
A program may use at most 2 GiB of HBM per device.

v0:
```python
import jax
import jax.numpy as jnp


def solution(mesh):
    def step(x, w_gate, w_up, w_down):
        gate, up = jnp.dot(x, w_gate), jnp.dot(x, w_up)
        hidden = (jax.nn.silu(gate.astype(jnp.float32)) * up.astype(jnp.float32)).astype(jnp.bfloat16)
        return jnp.dot(hidden, w_down)

    return step
```

profile of v0, /device:TPU:0, one launch (start us, length us, event | category | flops | bytes accessed | tf_op | source)
XLA Modules:
  0.0 1561.1 jit_solution(3544429712821347348)
XLA Ops:
  6.5 0.0 all-gather.4.cloned.1.call-start
  6.5 0.7 all-gather.4.cloned.1.call-update
  7.3 0.0 all-reduce.7.cloned.1.call-start
  7.3 108.6 %all-gather.4.cloned.1.call-done = bf16[2048,4096]{1,0:T(8,128)(2,1)} async-done(((bf16[2048,1024]{1,0:T(8,128)(2,1)}), bf16[2048,4096]{1,0:T(8,128)(2,1)}) %all-gather.4.cloned.1.call-update) | async-done | bytes 16777232 | tf_op args[0]
  115.9 0.0 copy-start
  115.9 107.3 %fusion.9 = bf16[2048,5504]{1,0:T(8,128)(2,1)} fusion(bf16[2048,4096]{1,0:T(8,128)(2,1)} %all-gather.4.cloned.1.call-done, bf16[4096,5504]{1,0:T(8,128)(2,1)} %param.2), kind=kOutput, calls=%fused_computation.10 | convolution fusion | flops 92341796864 | bytes 84410368 | tf_op jit(solution)/dot_general | solution.py:7
  223.2 0.0 copy-done
  223.2 107.4 %fusion.8 = bf16[2048,5504]{1,0:T(8,128)(2,1)} fusion(bf16[2048,4096]{1,0:T(8,128)(2,1)S(1)} %copy-done, bf16[4096,5504]{1,0:T(8,128)(2,1)} %param.1), kind=kOutput, calls=%fused_computation.9 | convolution fusion | flops 92341796864 | bytes 84410368 | tf_op jit(solution)/dot_general | solution.py:7
  330.6 0.0 all-reduce.7.cloned.1.call-update
  330.6 0.0 reduce-scatter.4.cloned.1.call-start
  330.7 979.7 %all-reduce.7.cloned.1.call-done = (bf16[2048,5504]{1,0:T(8,128)(2,1)}, bf16[2048,5504]{1,0:T(8,128)(2,1)}) async-done(((bf16[2048,5504]{1,0:T(8,128)(2,1)}, bf16[2048,5504]{1,0:T(8,128)(2,1)}), (bf16[2048,5504]{1,0:T(8,128)(2,1)}, bf16[2048,5504]{1,0:T(8,128)(2,1)})) %all-reduce.7.cloned.1.call-update) | async-done | bytes 45088784 | tf_op jit(solution)/dot_general | solution.py:7
  1310.3 123.1 %fusion.5 = bf16[2048,4096]{1,0:T(8,128)(2,1)} fusion(bf16[5504,4096]{1,0:T(8,128)(2,1)} %param.3, bf16[2048,5504]{1,0:T(8,128)(2,1)} %get-tuple-element.4, bf16[2048,5504]{1,0:T(8,128)(2,1)} %get-tuple-element.5), kind=kOutput, calls=%fused_computation.7 | convolution fusion | flops 92431974400 | bytes 106954752 | tf_op jit(solution)/dot_general | solution.py:9
  1433.4 0.0 reduce-scatter.4.cloned.1.call-update
  1433.5 121.1 %reduce-scatter.4.cloned.1.call-done = bf16[2048,1024]{1,0:T(8,128)(2,1)} async-done(((bf16[2048,4096]{1,0:T(8,128)(2,1)}), bf16[2048,1024]{1,0:T(8,128)(2,1)}) %reduce-scatter.4.cloned.1.call-update) | async-done | bytes 4194320
Async XLA Ops:
  6.5 109.4 %all-gather.4.cloned.1.call-start = ((), (), s32[]{:S(2)}) async-start(), calls=%async_computation.1 | async-start | bytes 20971520 | tf_op args[0]
  7.3 1303.1 %all-reduce.7.cloned.1.call-start = ((), (), s32[]{:S(2)}) async-start(), calls=%async_computation.3 | async-start | bytes 90177536 | tf_op jit(solution)/dot_general | solution.py:7
  115.9 107.3 %copy-start = (bf16[2048,4096]{1,0:T(8,128)(2,1)S(1)}, bf16[2048,4096]{1,0:T(8,128)(2,1)}, u32[]{:S(2)}) copy-start(bf16[2048,4096]{1,0:T(8,128)(2,1)} %all-gather.4.cloned.1.call-done) | copy-start | bytes 50331652
  330.6 1224.0 %reduce-scatter.4.cloned.1.call-start = ((), (), s32[]{:S(2)}) async-start(), calls=%async_computation.2 | async-start | bytes 20971520
Sparse Core Ops, SparseCore 0:
  8.9 107.0 all-gather.3
  330.8 979.5 all-reduce.6
  1433.6 120.9 reduce-scatter.3
where the time goes:
time: 1560 us
  waiting for transfers between devices  1210 us (78%)
  matrix products  338 us (22%)
    dot_general x1, waiting for transfers between devices, step(): gate, up = (jnp.dot(x, w_gate), jnp.dot(x, w_up))  980 us
    unnamed x5, waiting for transfers between devices  230 us
    dot_general x2, matrix products, step(): gate, up = (jnp.dot(x, w_gate), jnp.dot(x, w_up))  215 us
    dot_general x1, matrix products, step(): return jnp.dot(hidden, w_down)  123 us
  transfers between devices with their start and end apart: 3, of which 3 were waited for; matrix products, arithmetic and copies ran while one was open for 0% of the time, Pallas kernels for 0%

commit v1 on v0

v1 whole, which is shorter than its diff:
```python
import functools

import jax
import jax.numpy as jnp
from jax import lax
from jax.experimental import pallas as pl
from jax.experimental.pallas import tpu as pltpu
from jax.sharding import PartitionSpec as P

BLOCK = 128
WIDE = 256
LANES = 128
LAG_E, LAG_D = 3, 6
RING = 8
KEPT = LAG_E + 1
WEIGHTS = 3
F32, BF16 = jnp.float32, jnp.bfloat16


def dot(p, q):
    return jnp.dot(p, q, preferred_element_type=F32)


def kernel(n, wide, x, wg, wu, wd, out, xg, wbuf, dbuf, acc, mine, psend, precv, hbuf, ysend, yrecv, yown, yout,
           x_own, x_send, x_recv, w_sem, d_sem, p_send, p_recv, q_send, q_recv, y_send, y_recv, o_sem):
    rows, depth = x.shape
    ff = wg.shape[1]
    half = rows // 2
    blocks = half // n
    tiles = -(-ff // wide)
    last = ff - (tiles - 1) * wide
    steps = blocks * tiles
    cut = depth
    a, b = lax.axis_index("a"), lax.axis_index("b")
    peers = [lax.rem(b + k, 4) for k in range(4)]
    partner = {"a": 1 - a}

    def rows_of(s, part):
        owner = a if part == 0 else 1 - a
        return pl.ds(pl.multiple_of(owner * half + s * n, n), n)

    def by_width(u, run):
        c = lax.rem(u, tiles)
        if last == wide:
            run(wide)
            return

        @pl.when(c != tiles - 1)
        def _():
            run(wide)

        @pl.when(c == tiles - 1)
        def _():
            run(last)

    def remote(src, dst, send, recv, to):
        return pltpu.make_async_remote_copy(
            src_ref=src, dst_ref=dst, send_sem=send, recv_sem=recv, device_id=to,
            device_id_type=pl.DeviceIdType.MESH)

    def x_local(s, part):
        return pltpu.make_async_copy(
            x.at[rows_of(s, part)], xg.at[s, pl.ds(part * n, n), pl.ds(0, depth)], x_own.at[s, part])

    def x_remote(s, part, k):
        return remote(
            x.at[rows_of(s, part)], xg.at[s, pl.ds(part * n, n), pl.ds((4 - k) * depth, depth)],
            x_send.at[s, part, k - 1], x_recv.at[s, part, 3 - k], {"b": peers[k]})

    def w_copies(u, width):
        slot = lax.rem(u, WEIGHTS)
        start = lax.rem(u, tiles) * wide
        columns = pl.ds(pl.multiple_of(start, LANES), width)
        copies = []
        for k in range(4):
            deep = pl.ds(pl.multiple_of(peers[k] * depth, depth), depth)
            for i, w in enumerate((wg, wu)):
                copies.append(pltpu.make_async_copy(
                    w.at[deep, columns],
                    wbuf.at[slot, pl.ds(k * depth, depth), pl.ds(i * width, width)], w_sem.at[slot, k, i]))
        return copies

    def d_copies(u, width):
        slot = lax.rem(u, WEIGHTS)
        start = lax.rem(u, tiles) * wide
        deep = pl.ds(pl.multiple_of(start, LANES), width)
        return [
            pltpu.make_async_copy(
                wd.at[deep, pl.ds(pl.multiple_of(peers[k] * cut, cut), cut)],
                dbuf.at[slot, k, pl.ds(0, width)], d_sem.at[slot, k])
            for k in range(4)]

    def start_all(copies):
        for copy in copies:
            copy.start()

    def wait_all(copies):
        for copy in copies:
            copy.wait()

    def p_copy(u, width):
        slot = lax.rem(u, RING)
        return remote(psend.at[slot, :, pl.ds(0, 2 * width)], precv.at[slot, :, pl.ds(0, 2 * width)],
                      p_send.at[slot], p_recv.at[slot], partner)

    def q_copy(u, width):
        slot = lax.rem(u, RING)
        return remote(hbuf.at[slot, pl.ds(0, n), pl.ds(0, width)], hbuf.at[slot, pl.ds(n, n), pl.ds(0, width)],
                      q_send.at[slot], q_recv.at[slot], partner)

    def y_copy(s, k):
        return remote(ysend.at[k - 1], yrecv.at[lax.rem(s, 2), 3 - k],
                      y_send.at[k - 1], y_recv.at[lax.rem(s, 2), 3 - k], {"b": peers[k]})

    def o_copy(s, part):
        return pltpu.make_async_copy(yout.at[pl.ds(part * n, n)], out.at[rows_of(s, part)], o_sem.at[part])

    def partial_sums(t):
        s, c = t // tiles, lax.rem(t, tiles)

        @pl.when(t + WEIGHTS - 1 < steps)
        def _():
            by_width(t + WEIGHTS - 1, lambda width: start_all(w_copies(t + WEIGHTS - 1, width)))

        @pl.when(c == 0)
        def _():
            for part in range(2):
                x_local(s, part).wait()
                for k in range(1, 4):
                    x_remote(s, part, k).wait_recv()

        @pl.when(t >= RING)
        def _():
            by_width(t - RING, lambda width: p_copy(t - RING, width).wait_send())

        def run(width):
            wait_all(w_copies(t, width))
            total = dot(xg[s], wbuf[lax.rem(t, WEIGHTS), :, : 2 * width])
            psend[lax.rem(t, RING), :, : 2 * width] = total[n:].astype(BF16)
            mine[lax.rem(t, KEPT), :, : 2 * width] = total[:n]
            p_copy(t, width).start()

        by_width(t, run)

    def hidden(u):
        @pl.when(u >= RING)
        def _():
            by_width(u - RING, lambda width: q_copy(u - RING, width).wait_send())

        def run(width):
            p_copy(u, width).wait_recv()
            slot, kept = lax.rem(u, RING), lax.rem(u, KEPT)
            gate = mine[kept, :, :width] + precv[slot, :, :width].astype(F32)
            up = mine[kept, :, width : 2 * width] + precv[slot, :, width : 2 * width].astype(F32)
            hbuf[slot, :n, :width] = (jax.nn.silu(gate) * up).astype(BF16)
            q_copy(u, width).start()

        by_width(u, run)

    def hand_out(s):
        @pl.when(s > 0)
        def _():
            for k in range(1, 4):
                y_copy(s - 1, k).wait_send()

        for k in range(1, 4):
            ysend[k - 1] = acc[k].astype(BF16)
            y_copy(s, k).start()
        yown[...] = acc[0]
        acc[...] = jnp.zeros_like(acc)

    def finish(s):
        for k in range(1, 4):
            y_copy(s, k).wait_recv()

        @pl.when(s > 0)
        def _():
            for part in range(2):
                o_copy(s - 1, part).wait()

        slot = lax.rem(s, 2)
        total = yown[...]
        for k in range(3):
            total = total + yrecv[slot, k].astype(F32)
        yout[...] = total.astype(BF16)
        for part in range(2):
            o_copy(s, part).start()

    def down(u):
        s, c = u // tiles, lax.rem(u, tiles)

        @pl.when(u + WEIGHTS - 1 < steps)
        def _():
            by_width(u + WEIGHTS - 1, lambda width: start_all(d_copies(u + WEIGHTS - 1, width)))

        def run(width):
            wait_all(d_copies(u, width))
            q_copy(u, width).wait_recv()
            h = hbuf[lax.rem(u, RING), :, :width]
            for k in range(4):
                acc[k] += dot(h, dbuf[lax.rem(u, WEIGHTS), k, :width])

        by_width(u, run)

        @pl.when(c == tiles - 1)
        def _():
            hand_out(s)

        @pl.when((c == tiles // 2) & (s > 0))
        def _():
            finish(s - 1)

    barrier = pltpu.get_barrier_semaphore()
    for to in [partner] + [{"b": peers[k]} for k in range(1, 4)]:
        pl.semaphore_signal(barrier, inc=1, device_id=to, device_id_type=pl.DeviceIdType.MESH)
    for u in range(WEIGHTS - 1):
        start_all(w_copies(u, wide))
        start_all(d_copies(u, wide))

    def own(s, _):
        for part in range(2):
            x_local(s, part).start()
        return 0

    lax.fori_loop(0, blocks, own, 0)
    acc[...] = jnp.zeros_like(acc)
    pl.semaphore_wait(barrier, 4)

    def others(s, _):
        for part in range(2):
            for k in range(1, 4):
                x_remote(s, part, k).start()
        return 0

    lax.fori_loop(0, blocks, others, 0)

    def step(t, _):
        @pl.when(t < steps)
        def _():
            partial_sums(t)

        @pl.when((t >= LAG_E) & (t < steps + LAG_E))
        def _():
            hidden(t - LAG_E)

        @pl.when(t >= LAG_D)
        def _():
            down(t - LAG_D)

        return 0

    lax.fori_loop(0, steps + LAG_D, step, 0)
    finish(blocks - 1)
    for part in range(2):
        o_copy(blocks - 1, part).wait()
    for k in range(1, 4):
        y_copy(blocks - 1, k).wait_send()
    for u in range(steps - RING, steps):
        width = last if u % tiles == tiles - 1 else wide
        p_copy(u, width).wait_send()
        q_copy(u, width).wait_send()

    def sent(s, _):
        for part in range(2):
            for k in range(1, 4):
                x_remote(s, part, k).wait_send()
        return 0

    lax.fori_loop(0, blocks, sent, 0)


def solution(mesh, n=BLOCK, wide=WIDE):
    def body(x, w_gate, w_up, w_down):
        rows, depth = x.shape
        blocks = rows // 2 // n
        dma = pltpu.SemaphoreType.DMA
        return pl.pallas_call(
            functools.partial(kernel, n, wide),
            out_shape=jax.ShapeDtypeStruct(x.shape, BF16),
            in_specs=[pl.BlockSpec(memory_space=pl.ANY)] * 4,
            out_specs=pl.BlockSpec(memory_space=pl.ANY),
            scratch_shapes=[
                pltpu.VMEM((blocks, 2 * n, 4 * depth), BF16),
                pltpu.VMEM((WEIGHTS, 4 * depth, 2 * wide), BF16),
                pltpu.VMEM((WEIGHTS, 4, wide, depth), BF16),
                pltpu.VMEM((4, 2 * n, depth), F32),
                pltpu.VMEM((KEPT, n, 2 * wide), F32),
                pltpu.VMEM((RING, n, 2 * wide), BF16),
                pltpu.VMEM((RING, n, 2 * wide), BF16),
                pltpu.VMEM((RING, 2 * n, wide), BF16),
                pltpu.VMEM((3, 2 * n, depth), BF16),
                pltpu.VMEM((2, 3, 2 * n, depth), BF16),
                pltpu.VMEM((2 * n, depth), F32),
                pltpu.VMEM((2 * n, depth), BF16),
                dma((blocks, 2)), dma((blocks, 2, 3)), dma((blocks, 2, 3)),
                dma((WEIGHTS, 4, 2)), dma((WEIGHTS, 4)),
                dma((RING,)), dma((RING,)), dma((RING,)), dma((RING,)),
                dma((3,)), dma((2, 3)), dma((2,)),
            ],
            compiler_params=pltpu.CompilerParams(
                collective_id=0, has_side_effects=True, vmem_limit_bytes=67_000_000),
        )(x, w_gate, w_up, w_down)

    return jax.shard_map(
        body,
        mesh=mesh,
        in_specs=(P("dp", ("a", "b")), P("a", "b"), P("a", "b"), P("b", "a")),
        out_specs=P("dp", ("a", "b")),
        check_vma=False,
    )
```

time: 1560 us -> 787 us (0.50)
  waiting for transfers between devices: 1210 us -> 0 us
  Pallas kernels: 0 us -> 778 us
  matrix products: 338 us -> 0 us
    dot_general x1 -> x0, waiting for transfers between devices: 980 us -> none  [step(): gate, up = (jnp.dot(x, w_gate), jnp.dot(x, w_up))]
    pallas_call x0 -> x1, Pallas kernels: none -> 778 us  [body(): pl.pallas_call(functools.partial(kernel, n, wide), out_shape=jax.ShapeDty...]
    dot_general x3 -> x0, matrix products: 338 us -> none  [the longest x2 215 us: step(): gate, up = (jnp.dot(x, w_gate), jnp.dot(x, w_up))]
    unnamed x5 -> x0, waiting for transfers between devices: 230 us -> none
  transfers between devices with their start and end apart: 3 -> 0, of which waited for: 3 -> 0; matrix products, arithmetic and copies ran while one was open for 0% -> 0% of each run, Pallas kernels for 0% -> 0%
where the time goes in v1:
time: 787 us; the launch traced here: 783 us
  Pallas kernels  778 us (99%)
    pallas_call x1, Pallas kernels, body(): pl.pallas_call(functools.partial(kernel, n, wide), out_shape=jax.ShapeDty...  778 us

profile of v1, /device:TPU:0, one launch (start us, length us, event | category | flops | bytes accessed | tf_op | source)
XLA Modules:
  0.0 782.7 jit_solution(6070487300739291243)
XLA Ops:
  0.0 778.0 %shard_map.46 = bf16[2048,1024]{1,0:T(8,128)(2,1)} custom-call(bf16[2048,1024]{1,0:T(8,128)(2,1)} %x.1, bf16[4096,5504]{1,0:T(8,128)(2,1)} %wg.1, bf16[4096,5504]{1,0:T(8,128)(2,1)} %wu.1, bf16[5504,4096]{1,0:T(8,128)(2,1)} %wd.1), custom_call_target="tpu_custom_call" | custom-call | tf_op jit(solution)/shard_map/pallas_call | solution.py:277
  778.0 4.6 copy.6

commit v2 on v1

v2 whole, which is shorter than its diff:
```python
import functools

import jax
import jax.numpy as jnp
from jax import lax
from jax.experimental import pallas as pl
from jax.experimental.pallas import tpu as pltpu
from jax.sharding import PartitionSpec as P

BLOCK = 128
WIDE = 256
LANES = 128
LAG_E, LAG_D = 3, 6
RING = 8
KEPT = LAG_E + 1
WEIGHTS = 3
F32, BF16 = jnp.float32, jnp.bfloat16


def dot(p, q):
    return jnp.dot(p, q, preferred_element_type=F32)


def kernel(n, wide, x, wg, wu, wd, out, xg, wbuf, dbuf, acc, mine, psend, precv, hbuf, ysend, yrecv, zsend, zrecv,
           yown, ykeep, yout, x_own, x_send, x_recv, w_sem, d_sem, p_send, p_recv, q_send, q_recv, y_send, y_recv,
           z_send, z_recv, o_sem):
    rows, depth = x.shape
    ff = wg.shape[1]
    half = rows // 2
    small = n // 2
    blocks = half // n + 1
    tiles = -(-ff // wide)
    last = ff - (tiles - 1) * wide
    steps = blocks * tiles
    cut = depth
    a, b = lax.axis_index("a"), lax.axis_index("b")
    chip, core = b // 2, lax.rem(b, 2)
    peers = [b, chip * 2 + 1 - core, (1 - chip) * 2 + core, (1 - chip) * 2 + 1 - core]
    partner, mate, across = {"a": 1 - a}, {"b": peers[1]}, {"b": peers[2]}

    def first_row(s):
        return s * n - small * ((s + blocks - 1) // blocks)

    def rows_of(s, part, size):
        owner = a if part == 0 else 1 - a
        return pl.ds(pl.multiple_of(owner * half + first_row(s), small), size)

    def held(s, start, size):
        return pl.ds(pl.multiple_of(2 * first_row(s) + start, small), size)

    def by_rows(s, run):
        if isinstance(s, int):
            return run(small if s in (0, blocks - 1) else n)
        ends = (s == 0) | (s == blocks - 1)

        @pl.when(ends)
        def _():
            run(small)

        @pl.when(jnp.logical_not(ends))
        def _():
            run(n)

    def by_width(u, run):
        if isinstance(u, int):
            return run(last if u % tiles == tiles - 1 else wide)
        c = lax.rem(u, tiles)
        if last == wide:
            return run(wide)

        @pl.when(c != tiles - 1)
        def _():
            run(wide)

        @pl.when(c == tiles - 1)
        def _():
            run(last)

    def by_shape(u, run):
        by_rows(u // tiles, lambda size: by_width(u, lambda width: run(size, width)))

    def remote(src, dst, send, recv, to):
        return pltpu.make_async_remote_copy(
            src_ref=src, dst_ref=dst, send_sem=send, recv_sem=recv, device_id=to,
            device_id_type=pl.DeviceIdType.MESH)

    def x_copy(s, part, k, size):
        to = held(s, part * size, size)
        if k == 0:
            return pltpu.make_async_copy(x.at[rows_of(s, part, size)], xg.at[to, pl.ds(0, depth)], x_own.at[s, part])
        src = xg.at[to, pl.ds(2 * depth, depth)] if k == 3 else x.at[rows_of(s, part, size)]
        return remote(src, xg.at[to, pl.ds(k * depth, depth)], x_send.at[s, part, k - 1], x_recv.at[s, part, k - 1],
                      across if k == 2 else mate)

    def x_start(s, k):
        by_rows(s, lambda size: [x_copy(s, part, k, size).start() for part in range(2)])

    def x_forward(s):
        def run(size):
            for part in range(2):
                x_copy(s, part, 2, size).wait_recv()
                x_copy(s, part, 3, size).start()

        by_rows(s, run)

    def w_copies(u, width):
        slot = lax.rem(u, WEIGHTS)
        start = lax.rem(u, tiles) * wide
        columns = pl.ds(pl.multiple_of(start, LANES), width)
        copies = []
        for k in range(4):
            deep = pl.ds(pl.multiple_of(peers[k] * depth, depth), depth)
            for i, w in enumerate((wg, wu)):
                copies.append(pltpu.make_async_copy(
                    w.at[deep, columns],
                    wbuf.at[slot, pl.ds(k * depth, depth), pl.ds(i * width, width)], w_sem.at[slot, k, i]))
        return copies

    def d_copies(u, width):
        slot = lax.rem(u, WEIGHTS)
        start = lax.rem(u, tiles) * wide
        deep = pl.ds(pl.multiple_of(start, LANES), width)
        return [
            pltpu.make_async_copy(
                wd.at[deep, pl.ds(pl.multiple_of(peers[k] * cut, cut), cut)],
                dbuf.at[slot, k, pl.ds(0, width)], d_sem.at[slot, k])
            for k in range(4)]

    def start_all(copies):
        for copy in copies:
            copy.start()

    def wait_all(copies):
        for copy in copies:
            copy.wait()

    def p_copy(u, size, width):
        slot = lax.rem(u, RING)
        part = (slot, pl.ds(0, size), pl.ds(0, 2 * width))
        return remote(psend.at[part], precv.at[part], p_send.at[slot], p_recv.at[slot], partner)

    def q_copy(u, size, width):
        slot = lax.rem(u, RING)
        return remote(hbuf.at[slot, pl.ds(0, size), pl.ds(0, width)], hbuf.at[slot, pl.ds(size, size), pl.ds(0, width)],
                      q_send.at[slot], q_recv.at[slot], partner)

    def y_copy(s, i, size):
        slot = lax.rem(s, 2)
        return remote(ysend.at[i, pl.ds(0, 2 * size)], yrecv.at[slot, i, pl.ds(0, 2 * size)],
                      y_send.at[i], y_recv.at[slot, i], mate)

    def z_copy(s, size):
        slot = lax.rem(s, 2)
        return remote(zsend.at[pl.ds(0, 2 * size)], zrecv.at[slot, pl.ds(0, 2 * size)], z_send, z_recv.at[slot], across)

    def o_copy(s, part, size):
        return pltpu.make_async_copy(yout.at[pl.ds(part * size, size)], out.at[rows_of(s, part, size)], o_sem.at[part])

    def partial_sums(t):
        s, c = t // tiles, lax.rem(t, tiles)

        @pl.when(t + WEIGHTS - 1 < steps)
        def _():
            by_width(t + WEIGHTS - 1, lambda width: start_all(w_copies(t + WEIGHTS - 1, width)))

        @pl.when((c == tiles // 2) & (s + 1 < blocks))
        def _():
            x_forward(s + 1)

        @pl.when(c == 0)
        def _():
            def run(size):
                for part in range(2):
                    x_copy(s, part, 0, size).wait()
                    x_copy(s, part, 1, size).wait_recv()
                    x_copy(s, part, 3, size).wait_recv()

            by_rows(s, run)

        @pl.when(t >= RING)
        def _():
            by_shape(t - RING, lambda size, width: p_copy(t - RING, size, width).wait_send())
            by_shape(t - RING, lambda size, width: q_copy(t - RING, size, width).wait_send())

        def run(size, width):
            wait_all(w_copies(t, width))
            total = dot(xg[held(s, 0, 2 * size)], wbuf[lax.rem(t, WEIGHTS), :, : 2 * width])
            psend[lax.rem(t, RING), :size, : 2 * width] = total[size:].astype(BF16)
            mine[lax.rem(t, KEPT), :size, : 2 * width] = total[:size]
            p_copy(t, size, width).start()

        by_shape(t, run)

    def hidden(u):
        def run(size, width):
            p_copy(u, size, width).wait_recv()
            slot, kept = lax.rem(u, RING), lax.rem(u, KEPT)
            gate = mine[kept, :size, :width] + precv[slot, :size, :width].astype(F32)
            up = mine[kept, :size, width : 2 * width] + precv[slot, :size, width : 2 * width].astype(F32)
            hbuf[slot, :size, :width] = (jax.nn.silu(gate) * up).astype(BF16)
            q_copy(u, size, width).start()

        by_shape(u, run)

    def hand_out(s):
        @pl.when(s > 0)
        def _():
            by_rows(s - 1, lambda size: [y_copy(s - 1, i, size).wait_send() for i in range(2)])

        def run(size):
            for i in (1, 0):
                ysend[i, : 2 * size] = acc[2 * i + 1, : 2 * size].astype(BF16)
                y_copy(s, i, size).start()
            yown[: 2 * size] = acc[0, : 2 * size]
            ykeep[: 2 * size] = acc[2, : 2 * size]

        by_rows(s, run)
        acc[...] = jnp.zeros_like(acc)

    def pass_on(s):
        def run(size):
            y_copy(s, 1, size).wait_recv()
            total = ykeep[: 2 * size] + yrecv[lax.rem(s, 2), 1, : 2 * size].astype(F32)
            zsend[: 2 * size] = total.astype(BF16)
            z_copy(s, size).start()

        by_rows(s, run)

    def finish(s):
        def written(size):
            for part in range(2):
                o_copy(s - 1, part, size).wait()

        if isinstance(s, int):
            by_rows(s - 1, written)
        else:
            pl.when(s > 0)(lambda: by_rows(s - 1, written))

        def run(size):
            slot = lax.rem(s, 2)
            y_copy(s, 0, size).wait_recv()
            total = yown[: 2 * size] + yrecv[slot, 0, : 2 * size].astype(F32)
            z_copy(s, size).wait_recv()
            yout[: 2 * size] = (total + zrecv[slot, : 2 * size].astype(F32)).astype(BF16)
            for part in range(2):
                o_copy(s, part, size).start()
            z_copy(s, size).wait_send()

        by_rows(s, run)

    def down(u):
        s, c = u // tiles, lax.rem(u, tiles)

        @pl.when(u + WEIGHTS - 1 < steps)
        def _():
            by_width(u + WEIGHTS - 1, lambda width: start_all(d_copies(u + WEIGHTS - 1, width)))

        def run(size, width):
            wait_all(d_copies(u, width))
            q_copy(u, size, width).wait_recv()
            h = hbuf[lax.rem(u, RING), : 2 * size, :width]
            for k in range(4):
                acc[k, : 2 * size] += dot(h, dbuf[lax.rem(u, WEIGHTS), k, :width])

        by_shape(u, run)

        @pl.when(c == tiles - 1)
        def _():
            hand_out(s)

        @pl.when((c == 1) & (s > 0))
        def _():
            pass_on(s - 1)

        @pl.when((c == tiles // 2) & (s > 0))
        def _():
            finish(s - 1)

    barrier = pltpu.get_barrier_semaphore()
    for to in (partner, mate, across):
        pl.semaphore_signal(barrier, inc=1, device_id=to, device_id_type=pl.DeviceIdType.MESH)

    def each(low, run):
        def one(s, _):
            run(s)
            return 0

        lax.fori_loop(low, blocks, one, 0)

    each(0, lambda s: x_start(s, 0))
    for u in range(WEIGHTS - 1):
        start_all(w_copies(u, wide))
    acc[...] = jnp.zeros_like(acc)
    pl.semaphore_wait(barrier, 3)
    x_start(0, 2)
    x_start(0, 1)
    each(1, lambda s: x_start(s, 2))
    for u in range(WEIGHTS - 1):
        start_all(d_copies(u, wide))
    x_forward(0)
    each(1, lambda s: x_start(s, 1))

    def step(t, _):
        @pl.when(t < steps)
        def _():
            partial_sums(t)

        @pl.when((t >= LAG_E) & (t < steps + LAG_E))
        def _():
            hidden(t - LAG_E)

        @pl.when(t >= LAG_D)
        def _():
            down(t - LAG_D)

        return 0

    lax.fori_loop(0, steps + LAG_D, step, 0)
    end = blocks - 1
    pass_on(end)
    finish(end)
    for part in range(2):
        o_copy(end, part, small).wait()
    for i in range(2):
        y_copy(end, i, small).wait_send()
    for u in range(steps - RING, steps):
        by_shape(u, lambda size, width: p_copy(u, size, width).wait_send())
        by_shape(u, lambda size, width: q_copy(u, size, width).wait_send())
    for k in range(1, 4):
        each(0, lambda s: by_rows(s, lambda size: [x_copy(s, part, k, size).wait_send() for part in range(2)]))


def solution(mesh, n=BLOCK, wide=WIDE):
    def body(x, w_gate, w_up, w_down):
        rows, depth = x.shape
        blocks = rows // 2 // n + 1
        dma = pltpu.SemaphoreType.DMA
        return pl.pallas_call(
            functools.partial(kernel, n, wide),
            out_shape=jax.ShapeDtypeStruct(x.shape, BF16),
            in_specs=[pl.BlockSpec(memory_space=pl.ANY)] * 4,
            out_specs=pl.BlockSpec(memory_space=pl.ANY),
            scratch_shapes=[
                pltpu.VMEM((rows, 4 * depth), BF16),
                pltpu.VMEM((WEIGHTS, 4 * depth, 2 * wide), BF16),
                pltpu.VMEM((WEIGHTS, 4, wide, depth), BF16),
                pltpu.VMEM((4, 2 * n, depth), F32),
                pltpu.VMEM((KEPT, n, 2 * wide), F32),
                pltpu.VMEM((RING, n, 2 * wide), BF16),
                pltpu.VMEM((RING, n, 2 * wide), BF16),
                pltpu.VMEM((RING, 2 * n, wide), BF16),
                pltpu.VMEM((2, 2 * n, depth), BF16),
                pltpu.VMEM((2, 2, 2 * n, depth), BF16),
                pltpu.VMEM((2 * n, depth), BF16),
                pltpu.VMEM((2, 2 * n, depth), BF16),
                pltpu.VMEM((2 * n, depth), F32),
                pltpu.VMEM((2 * n, depth), F32),
                pltpu.VMEM((2 * n, depth), BF16),
                dma((blocks, 2)), dma((blocks, 2, 3)), dma((blocks, 2, 3)),
                dma((WEIGHTS, 4, 2)), dma((WEIGHTS, 4)),
                dma((RING,)), dma((RING,)), dma((RING,)), dma((RING,)),
                dma((2,)), dma((2, 2)), dma, dma((2,)), dma((2,)),
            ],
            compiler_params=pltpu.CompilerParams(
                collective_id=0, has_side_effects=True, vmem_limit_bytes=67_000_000),
        )(x, w_gate, w_up, w_down)

    return jax.shard_map(
        body,
        mesh=mesh,
        in_specs=(P("dp", ("a", "b")), P("a", "b"), P("a", "b"), P("b", "a")),
        out_specs=P("dp", ("a", "b")),
        check_vma=False,
    )
```

time: 787 us -> 757 us (0.962)
  Pallas kernels: 778 us -> 752 us
    pallas_call x1, Pallas kernels: 778 us -> 752 us  [body(): pl.pallas_call(functools.partial(kernel, n, wide), out_shape=jax.ShapeDty...]
where the time goes in v2:
time: 757 us
  Pallas kernels  752 us (99%)
    pallas_call x1, Pallas kernels, body(): pl.pallas_call(functools.partial(kernel, n, wide), out_shape=jax.ShapeDty...  752 us

profile of v2, /device:TPU:0, one launch (start us, length us, event | category | flops | bytes accessed | tf_op | source)
XLA Modules:
  0.0 756.9 jit_solution(6511463526138357364)
XLA Ops:
  0.0 752.2 %shard_map.46 = bf16[2048,1024]{1,0:T(8,128)(2,1)} custom-call(bf16[2048,1024]{1,0:T(8,128)(2,1)} %x.1, bf16[4096,5504]{1,0:T(8,128)(2,1)} %wg.1, bf16[4096,5504]{1,0:T(8,128)(2,1)} %wu.1, bf16[5504,4096]{1,0:T(8,128)(2,1)} %wd.1), custom_call_target="tpu_custom_call" | custom-call | tf_op jit(solution)/shard_map/pallas_call | solution.py:338
  752.2 4.6 copy.6

commit v3 on v2

--- a/solution.py
+++ b/solution.py
@@ -13,6 +13,7 @@
 LAG_E, LAG_D = 3, 6
 RING = 8
 KEPT = LAG_E + 1
+EARLY = 2
 WEIGHTS = 3
 F32, BF16 = jnp.float32, jnp.bfloat16
 
@@ -22,8 +23,8 @@
 
 
 def kernel(n, wide, x, wg, wu, wd, out, xg, wbuf, dbuf, acc, mine, psend, precv, hbuf, ysend, yrecv, zsend, zrecv,
-           yown, ykeep, yout, x_own, x_send, x_recv, w_sem, d_sem, p_send, p_recv, q_send, q_recv, y_send, y_recv,
-           z_send, z_recv, o_sem):
+           yown, ykeep, x_own, x_send, x_recv, w_sem, d_sem, p_send, p_recv, q_send, q_recv, y_send, y_recv,
+           z_send, z_recv):
     rows, depth = x.shape
     ff = wg.shape[1]
     half = rows // 2
@@ -92,14 +93,23 @@
         return remote(src, xg.at[to, pl.ds(k * depth, depth)], x_send.at[s, part, k - 1], x_recv.at[s, part, k - 1],
                       across if k == 2 else mate)
 
-    def x_start(s, k):
-        by_rows(s, lambda size: [x_copy(s, part, k, size).start() for part in range(2)])
-
-    def x_forward(s):
-        def run(size):
-            for part in range(2):
+    def x_start(s, k, parts=(0, 1)):
+        by_rows(s, lambda size: [x_copy(s, part, k, size).start() for part in parts])
+
+    def x_forward(s, parts=(0, 1)):
+        def run(size):
+            for part in parts:
                 x_copy(s, part, 2, size).wait_recv()
                 x_copy(s, part, 3, size).start()
+
+        by_rows(s, run)
+
+    def x_ready(s, parts=(0, 1)):
+        def run(size):
+            for part in parts:
+                x_copy(s, part, 0, size).wait()
+                x_copy(s, part, 1, size).wait_recv()
+                x_copy(s, part, 3, size).wait_recv()
 
         by_rows(s, run)
 
@@ -146,20 +156,18 @@
 
     def y_copy(s, i, size):
         slot = lax.rem(s, 2)
-        return remote(ysend.at[i, pl.ds(0, 2 * size)], yrecv.at[slot, i, pl.ds(0, 2 * size)],
-                      y_send.at[i], y_recv.at[slot, i], mate)
-
-    def z_copy(s, size):
+        to = pl.ds(0, 2 * size) if i == 0 else pl.ds((i - 1) * size, size)
+        return remote(ysend.at[min(i, 1), to], yrecv.at[slot, min(i, 1), to], y_send.at[i], y_recv.at[slot, i], mate)
+
+    def z_copy(s, part, size):
         slot = lax.rem(s, 2)
-        return remote(zsend.at[pl.ds(0, 2 * size)], zrecv.at[slot, pl.ds(0, 2 * size)], z_send, z_recv.at[slot], across)
-
-    def o_copy(s, part, size):
-        return pltpu.make_async_copy(yout.at[pl.ds(part * size, size)], out.at[rows_of(s, part, size)], o_sem.at[part])
+        to = pl.ds(part * size, size)
+        return remote(zsend.at[to], zrecv.at[slot, to], z_send.at[part], z_recv.at[slot, part], across)
 
     def partial_sums(t):
         s, c = t // tiles, lax.rem(t, tiles)
 
-        @pl.when(t + WEIGHTS - 1 < steps)
+        @pl.when((t > EARLY) & (t + WEIGHTS - 1 < steps))
         def _():
             by_width(t + WEIGHTS - 1, lambda width: start_all(w_copies(t + WEIGHTS - 1, width)))
 
@@ -169,13 +177,7 @@
 
         @pl.when(c == 0)
         def _():
-            def run(size):
-                for part in range(2):
-                    x_copy(s, part, 0, size).wait()
-                    x_copy(s, part, 1, size).wait_recv()
-                    x_copy(s, part, 3, size).wait_recv()
-
-            by_rows(s, run)
+            x_ready(s)
 
         @pl.when(t >= RING)
         def _():
@@ -188,6 +190,19 @@
             psend[lax.rem(t, RING), :size, : 2 * width] = total[size:].astype(BF16)
             mine[lax.rem(t, KEPT), :size, : 2 * width] = total[:size]
             p_copy(t, size, width).start()
+
+        by_shape(t, run)
+
+    def early_sums(t, part):
+        def run(size, width):
+            if part:
+                wait_all(w_copies(t, width))
+            total = dot(xg[held(0, part * size, size)], wbuf[t, :, : 2 * width])
+            if part:
+                psend[t, :size, : 2 * width] = total.astype(BF16)
+                p_copy(t, size, width).start()
+            else:
+                mine[t, :size, : 2 * width] = total
 
         by_shape(t, run)
 
@@ -205,12 +220,15 @@
     def hand_out(s):
         @pl.when(s > 0)
         def _():
-            by_rows(s - 1, lambda size: [y_copy(s - 1, i, size).wait_send() for i in range(2)])
-
-        def run(size):
-            for i in (1, 0):
-                ysend[i, : 2 * size] = acc[2 * i + 1, : 2 * size].astype(BF16)
-                y_copy(s, i, size).start()
+            by_rows(s - 1, lambda size: [y_copy(s - 1, i, size).wait_send() for i in range(3)])
+
+        def run(size):
+            for part in range(2):
+                to = pl.ds(part * size, size)
+                ysend[1, to] = acc[3, to].astype(BF16)
+                y_copy(s, part + 1, size).start()
+            ysend[0, : 2 * size] = acc[1, : 2 * size].astype(BF16)
+            y_copy(s, 0, size).start()
             yown[: 2 * size] = acc[0, : 2 * size]
             ykeep[: 2 * size] = acc[2, : 2 * size]
 
@@ -219,32 +237,25 @@
 
     def pass_on(s):
         def run(size):
-            y_copy(s, 1, size).wait_recv()
-            total = ykeep[: 2 * size] + yrecv[lax.rem(s, 2), 1, : 2 * size].astype(F32)
-            zsend[: 2 * size] = total.astype(BF16)
-            z_copy(s, size).start()
+            for part in range(2):
+                to = pl.ds(part * size, size)
+                y_copy(s, part + 1, size).wait_recv()
+                zsend[to] = (ykeep[to] + yrecv[lax.rem(s, 2), 1, to].astype(F32)).astype(BF16)
+                z_copy(s, part, size).start()
 
         by_rows(s, run)
 
     def finish(s):
-        def written(size):
-            for part in range(2):
-                o_copy(s - 1, part, size).wait()
-
-        if isinstance(s, int):
-            by_rows(s - 1, written)
-        else:
-            pl.when(s > 0)(lambda: by_rows(s - 1, written))
-
         def run(size):
             slot = lax.rem(s, 2)
             y_copy(s, 0, size).wait_recv()
-            total = yown[: 2 * size] + yrecv[slot, 0, : 2 * size].astype(F32)
-            z_copy(s, size).wait_recv()
-            yout[: 2 * size] = (total + zrecv[slot, : 2 * size].astype(F32)).astype(BF16)
             for part in range(2):
-                o_copy(s, part, size).start()
-            z_copy(s, size).wait_send()
+                to = pl.ds(part * size, size)
+                z_copy(s, part, size).wait_recv()
+                total = yown[to] + yrecv[slot, 0, to].astype(F32) + zrecv[slot, to].astype(F32)
+                out[rows_of(s, part, size)] = total.astype(BF16)
+            for part in range(2):
+                z_copy(s, part, size).wait_send()
 
         by_rows(s, run)
 
@@ -288,16 +299,27 @@
         lax.fori_loop(low, blocks, one, 0)
 
     each(0, lambda s: x_start(s, 0))
-    for u in range(WEIGHTS - 1):
+    for u in range(WEIGHTS):
         start_all(w_copies(u, wide))
     acc[...] = jnp.zeros_like(acc)
     pl.semaphore_wait(barrier, 3)
-    x_start(0, 2)
-    x_start(0, 1)
-    each(1, lambda s: x_start(s, 2))
+    for k in (2, 1):
+        x_start(0, k, (1,))
+    for k in (2, 1):
+        x_start(0, k, (0,))
+    x_forward(0, (1,))
+    x_ready(0, (1,))
+    early_sums(0, 1)
+    x_forward(0, (0,))
+    for u in range(1, EARLY):
+        early_sums(u, 1)
+    x_ready(0, (0,))
+    for u in range(EARLY):
+        early_sums(u, 0)
+        start_all(w_copies(u + WEIGHTS, wide))
     for u in range(WEIGHTS - 1):
         start_all(d_copies(u, wide))
-    x_forward(0)
+    each(1, lambda s: x_start(s, 2))
     each(1, lambda s: x_start(s, 1))
 
     def step(t, _):
@@ -315,13 +337,11 @@
 
         return 0
 
-    lax.fori_loop(0, steps + LAG_D, step, 0)
+    lax.fori_loop(EARLY, steps + LAG_D, step, 0)
     end = blocks - 1
     pass_on(end)
     finish(end)
-    for part in range(2):
-        o_copy(end, part, small).wait()
-    for i in range(2):
+    for i in range(3):
         y_copy(end, i, small).wait_send()
     for u in range(steps - RING, steps):
         by_shape(u, lambda size, width: p_copy(u, size, width).wait_send())
@@ -337,9 +357,9 @@
         dma = pltpu.SemaphoreType.DMA
         return pl.pallas_call(
             functools.partial(kernel, n, wide),
-            out_shape=jax.ShapeDtypeStruct(x.shape, BF16),
+            out_shape=pltpu.VMEM(x.shape, BF16),
             in_specs=[pl.BlockSpec(memory_space=pl.ANY)] * 4,
-            out_specs=pl.BlockSpec(memory_space=pl.ANY),
+            out_specs=pl.BlockSpec(memory_space=pltpu.VMEM),
             scratch_shapes=[
                 pltpu.VMEM((rows, 4 * depth), BF16),
                 pltpu.VMEM((WEIGHTS, 4 * depth, 2 * wide), BF16),
@@ -355,14 +375,13 @@
                 pltpu.VMEM((2, 2 * n, depth), BF16),
                 pltpu.VMEM((2 * n, depth), F32),
                 pltpu.VMEM((2 * n, depth), F32),
-                pltpu.VMEM((2 * n, depth), BF16),
                 dma((blocks, 2)), dma((blocks, 2, 3)), dma((blocks, 2, 3)),
                 dma((WEIGHTS, 4, 2)), dma((WEIGHTS, 4)),
                 dma((RING,)), dma((RING,)), dma((RING,)), dma((RING,)),
-                dma((2,)), dma((2, 2)), dma, dma((2,)), dma((2,)),
+                dma((3,)), dma((2, 3)), dma((2,)), dma((2, 2)),
             ],
             compiler_params=pltpu.CompilerParams(
-                collective_id=0, has_side_effects=True, vmem_limit_bytes=67_000_000),
+                collective_id=0, has_side_effects=True, vmem_limit_bytes=58_000_000),
         )(x, w_gate, w_up, w_down)
 
     return jax.shard_map(

time: 757 us -> 752 us (level)
  no operation moved by 1% of the time
where the time goes in v3:
time: 752 us
  Pallas kernels  750 us (100%)
    pallas_call x1, Pallas kernels, body(): pl.pallas_call(functools.partial(kernel, n, wide), out_shape=pltpu.VMEM(x...  750 us

profile of v3, /device:TPU:0, one launch (start us, length us, event | category | flops | bytes accessed | tf_op | source)
XLA Modules:
  0.0 752.3 jit_solution(10250660849511671150)
XLA Ops:
  0.0 750.3 %shard_map.46 = bf16[2048,1024]{1,0:T(8,128)(2,1)S(1)} custom-call(bf16[2048,1024]{1,0:T(8,128)(2,1)} %x.1, bf16[4096,5504]{1,0:T(8,128)(2,1)} %wg.1, bf16[4096,5504]{1,0:T(8,128)(2,1)} %wu.1, bf16[5504,4096]{1,0:T(8,128)(2,1)} %wd.1), custom_call_target="tpu_custom_call" | custom-call | tf_op jit(solution)/shard_map/pallas_call | solution.py:358
  750.3 2.0 copy.6

commit v4 on v3

--- a/solution.py
+++ b/solution.py
@@ -217,24 +217,6 @@
 
         by_shape(u, run)
 
-    def hand_out(s):
-        @pl.when(s > 0)
-        def _():
-            by_rows(s - 1, lambda size: [y_copy(s - 1, i, size).wait_send() for i in range(3)])
-
-        def run(size):
-            for part in range(2):
-                to = pl.ds(part * size, size)
-                ysend[1, to] = acc[3, to].astype(BF16)
-                y_copy(s, part + 1, size).start()
-            ysend[0, : 2 * size] = acc[1, : 2 * size].astype(BF16)
-            y_copy(s, 0, size).start()
-            yown[: 2 * size] = acc[0, : 2 * size]
-            ykeep[: 2 * size] = acc[2, : 2 * size]
-
-        by_rows(s, run)
-        acc[...] = jnp.zeros_like(acc)
-
     def pass_on(s):
         def run(size):
             for part in range(2):
@@ -270,14 +252,29 @@
             wait_all(d_copies(u, width))
             q_copy(u, size, width).wait_recv()
             h = hbuf[lax.rem(u, RING), : 2 * size, :width]
-            for k in range(4):
-                acc[k, : 2 * size] += dot(h, dbuf[lax.rem(u, WEIGHTS), k, :width])
+
+            def total(k):
+                return acc[k, : 2 * size] + dot(h, dbuf[lax.rem(u, WEIGHTS), k, :width])
+
+            if width == wide:
+                for k in range(4):
+                    acc[k, : 2 * size] = total(k)
+                return
+            across_sum = total(3).astype(BF16)
+            for part in range(2):
+                ysend[1, pl.ds(part * size, size)] = across_sum[part * size : (part + 1) * size]
+                y_copy(s, part + 1, size).start()
+            ysend[0, : 2 * size] = total(1).astype(BF16)
+            y_copy(s, 0, size).start()
+            ykeep[: 2 * size] = total(2)
+            yown[: 2 * size] = total(0)
+            acc[...] = jnp.zeros_like(acc)
+
+        @pl.when((c == tiles - 1) & (s > 0))
+        def _():
+            by_rows(s - 1, lambda size: [y_copy(s - 1, i, size).wait_send() for i in range(3)])
 
         by_shape(u, run)
-
-        @pl.when(c == tiles - 1)
-        def _():
-            hand_out(s)
 
         @pl.when((c == 1) & (s > 0))
         def _():
@@ -340,7 +337,6 @@
     lax.fori_loop(EARLY, steps + LAG_D, step, 0)
     end = blocks - 1
     pass_on(end)
-    finish(end)
     for i in range(3):
         y_copy(end, i, small).wait_send()
     for u in range(steps - RING, steps):
@@ -348,6 +344,7 @@
         by_shape(u, lambda size, width: q_copy(u, size, width).wait_send())
     for k in range(1, 4):
         each(0, lambda s: by_rows(s, lambda size: [x_copy(s, part, k, size).wait_send() for part in range(2)]))
+    finish(end)
 
 
 def solution(mesh, n=BLOCK, wide=WIDE):

time: 752 us -> 752 us (level)
  no operation moved by 1% of the time
where the time goes in v4:
time: 752 us
  Pallas kernels  750 us (100%)
    pallas_call x1, Pallas kernels, body(): pl.pallas_call(functools.partial(kernel, n, wide), out_shape=pltpu.VMEM(x...  750 us

profile of v4, /device:TPU:0, one launch (start us, length us, event | category | flops | bytes accessed | tf_op | source)
XLA Modules:
  0.0 752.3 jit_solution(13483771893939695992)
XLA Ops:
  0.0 750.2 %shard_map.46 = bf16[2048,1024]{1,0:T(8,128)(2,1)S(1)} custom-call(bf16[2048,1024]{1,0:T(8,128)(2,1)} %x.1, bf16[4096,5504]{1,0:T(8,128)(2,1)} %wg.1, bf16[4096,5504]{1,0:T(8,128)(2,1)} %wu.1, bf16[5504,4096]{1,0:T(8,128)(2,1)} %wd.1), custom_call_target="tpu_custom_call" | custom-call | tf_op jit(solution)/shard_map/pallas_call | solution.py:355
  750.3 2.0 copy.6
